TPU v7x, 32 devices: a whole 2x2x4 slice. The times are simulated.
32 devices in a mesh: row: 4 (over z), col: 8 (over y, x, core).
Axes of the slice: x: 2, y: 2, z: 4, core: 2. Of those that a mesh axis runs over, the one named last changes fastest.
Arguments:
- neighbor: int32 [32, 3072, 3072], P(None, 'col', 'row'), may hold values from 0 to 1, as said below
- true_coords: float32 [32, 3, 3072], P(None, None, ('row', 'col')), as said below
- pred_coords: float32 [32, 3, 3072], P(None, None, ('row', 'col')), as said below
- residue_mask: int32 [32, 3072], P(None, ('row', 'col')), may hold values from 0 to 1, as said below
- single: bfloat16 [32, 3072, 384], P(None, ('row', 'col'))
- ln_gain: float32 [384], replicated, may hold values from 0.1 to 1.9
- w_hidden: bfloat16 [384, 128], replicated, may hold values from -0.3125 to 0.3125
- b_hidden: float32 [128], replicated, may hold values from -3 to 3
- w_mid: bfloat16 [128, 128], replicated, may hold values from -0.5 to 0.5
- b_mid: float32 [128], replicated, may hold values from -3 to 3
- w_logits: bfloat16 [128, 50], replicated, may hold values from -1.5 to 1.5
- b_logits: float32 [50], replicated, may hold values from -4 to 4
Outputs:
- lddt_score: float32 [32, 3072], P(None, ('row', 'col'))
- residue_loss: float32 [32, 3072], P(None, ('row', 'col'))
- total_loss: float32 [], replicated
Inputs may be any that keep to these rules, and one draw needn't show every extreme that they name: `neighbor`: 0 or 1; 0 where j == i; 1 wherever 0 < |i - j| <= 8. `residue_mask`: per structure, 1 on a leading run of 1536 or more residues and 0 after it. `true_coords`: positions in angstroms. `pred_coords`: positions in angstroms.
All inputs are finite; a program needn't handle non-finite values.
Results may differ from a plain program's by a relative error of at most 0.00098.
Values sent between devices are 32-bit elements; how exact they have to be, the bound alone decides.
A program may use at most 128 MiB of HBM per device.

v0:
```python
import jax
import jax.numpy as jnp
from jax import lax
from jax.sharding import PartitionSpec as P

L = 3072
THRESHOLDS = (0.5, 1.0, 2.0, 4.0)


def from_root(shard, axis, root):
    mine = lax.axis_index(axis) == root
    return lax.psum(jnp.where(mine, shard, jnp.zeros_like(shard)), axis)


def tile_dist(rows_block, cols_block):
    total = (cols_block[:, 0, :, None] - rows_block[:, 0, None, :]) ** 2
    total = total + (cols_block[:, 1, :, None] - rows_block[:, 1, None, :]) ** 2
    total = total + (cols_block[:, 2, :, None] - rows_block[:, 2, None, :]) ** 2
    return jnp.sqrt(total + 1e-10)


def head_loss(lddt_value, single, ln_gain, w_hidden, b_hidden, w_mid, b_mid, w_logits, b_logits):
    features = single.astype(jnp.float32)
    average = jnp.mean(features, axis=-1, keepdims=True)
    centred = features - average
    variance = jnp.mean(centred * centred, axis=-1, keepdims=True)
    normed = (centred * lax.rsqrt(variance + 1e-05) * ln_gain).astype(jnp.bfloat16)
    first_hidden = jax.nn.relu(
        jnp.dot(normed, w_hidden, preferred_element_type=jnp.float32) + b_hidden
    ).astype(jnp.bfloat16)
    second_hidden = jax.nn.relu(
        jnp.dot(first_hidden, w_mid, preferred_element_type=jnp.float32) + b_mid
    ).astype(jnp.bfloat16)
    logits = jnp.dot(second_hidden, w_logits, preferred_element_type=jnp.float32) + b_logits
    log_total = jnp.log(jnp.sum(jnp.exp(logits), axis=-1))
    bins = logits.shape[-1]
    centers = (jnp.arange(bins).astype(jnp.float32) + 0.5) / bins
    closeness = jnp.exp(-((lddt_value[..., None] - centers) ** 2) * (bins * bins * 0.5))
    target = closeness / jnp.sum(closeness, axis=-1, keepdims=True)
    return log_total - jnp.sum(target * logits, axis=-1)


def local(
    neighbor,
    true_coords,
    pred_coords,
    residue_mask,
    single,
    ln_gain,
    w_hidden,
    b_hidden,
    w_mid,
    b_mid,
    w_logits,
    b_logits,
):
    valid = residue_mask.astype(jnp.float32)
    own_len = residue_mask.shape[1]
    stacked = jnp.concatenate([true_coords, pred_coords, valid[:, None, :]], axis=1)
    row_count = lax.axis_size("row")
    col_count = lax.axis_size("col")
    rows_len = L // row_count
    cols_len = L // col_count
    col_index = lax.axis_index("col")
    rows_part = lax.all_gather(stacked, "col", axis=2, tiled=True)
    offset = col_index * cols_len % rows_len
    column_piece = lax.dynamic_slice_in_dim(rows_part, offset, cols_len, 2)
    source_row = col_index * cols_len // rows_len
    cols_part = from_root(column_piece, "row", source_row)
    true_dist = tile_dist(rows_part[:, 0:3], cols_part[:, 0:3])
    pred_dist = tile_dist(rows_part[:, 3:6], cols_part[:, 3:6])
    mismatch = jnp.abs(pred_dist - true_dist)
    scores = jnp.zeros_like(mismatch)
    for threshold in THRESHOLDS:
        scores = scores + jax.nn.sigmoid(4.0 * (threshold - mismatch))
    scores = 0.25 * scores
    weights = neighbor.astype(jnp.float32) * rows_part[:, 6, None, :] * cols_part[:, 6, :, None]
    preserved = jnp.sum(weights * scores, axis=1)
    neighbors = jnp.sum(weights, axis=1)
    preserved_all, neighbors_all = lax.psum((preserved, neighbors), "col")
    preserved_own = lax.dynamic_slice_in_dim(preserved_all, col_index * own_len, own_len, 1)
    neighbors_own = lax.dynamic_slice_in_dim(neighbors_all, col_index * own_len, own_len, 1)
    lddt_score = preserved_own / jnp.maximum(neighbors_own, 1.0)
    residue_loss = valid * head_loss(
        lddt_score, single, ln_gain, w_hidden, b_hidden, w_mid, b_mid, w_logits, b_logits
    )
    loss_sum, valid_sum = lax.psum((jnp.sum(residue_loss), jnp.sum(valid)), ("row", "col"))
    total_loss = loss_sum / valid_sum
    return (lddt_score, residue_loss, total_loss)


def solution(mesh):
    placed = (
        P(None, "col", "row"),
        P(None, None, ("row", "col")),
        P(None, None, ("row", "col")),
        P(None, ("row", "col")),
        P(None, ("row", "col"), None),
        P(),
        P(),
        P(),
        P(),
        P(),
        P(),
        P(),
    )
    return jax.shard_map(
        local,
        mesh=mesh,
        in_specs=placed,
        out_specs=(P(None, ("row", "col")), P(None, ("row", "col")), P()),
        check_vma=False,
    )
```

profile of v0, /device:TPU:0, one launch (start us, length us, event | category | flops | bytes accessed | tf_op | source)
XLA Modules:
  0.0 312.7 jit_solution(15335422747212448188)
XLA Ops:
  7.2 0.0 copy-start
  7.2 0.0 all-reduce.5.cloned.1.call-start
  7.3 0.7 convert_bitcast_fusion
  8.0 0.8 pad_maximum_fusion
  8.8 0.9 copy.33
  9.7 21.3 %all_gather.3 = f32[32,7,768]{0,1,2:T(8,128)S(1)} all-gather(f32[32,7,96]{0,1,2:T(8,128)} %copy.33), channel_id=1, replica_groups=mesh['row'=4,'col'=8] {'col'}, dimensions={2}, use_global_device_ids=true | all-gather | bytes 774144 | tf_op jit(solution)/shard_map/all_gather | solution.py:65
  31.0 1.3 dynamic-slice_select_fusion
  32.3 0.0 all-reduce.5.cloned.1.call-update
  32.3 0.0 all-reduce.7.cloned.1.call-start
  32.4 3.3 %fusion.31 = (f32[32,1,768]{0,1,2:T(1,128)}, f32[32,1,768]{0,1,2:T(1,128)}, f32[32,1,768]{0,1,2:T(1,128)}, f32[32,1,768]{0,1,2:T(1,128)}, f32[32,1,768]{0,1,2:T(...) fusion(f32[32,7,768]{0,1,2:T(8,128)S(1)} %all_gather.3), kind=kLoop, calls=%fused_computation.43 | loop fusion | bytes 1376256 | tf_op jit(solution)/shard_map/slice | solution.py:77
  35.6 2.3 convert_reduce_fusion
  37.9 2.8 fusion.4
  40.8 0.0 copy-done
  40.8 3.2 %maximum_convert_fusion = bf16[32,96,128]{2,1,0:T(8,128)(2,1)S(1)} fusion(bf16[32,96,384]{2,1,0:T(8,128)(2,1)} %param.16, f32[384]{0:T(512)} %param.17, f32[32,96]{1,0:T(8,128)S(1)} %add_rsqrt_fusion, f32[32,96]{1,0:T(8,128)S(1)} %broadcast_multiply_fusion, f32[128]{0:T(128)} %param.21, f32[128]{0:T(128)} %param.19, bf16[384,128]{1,0:T(8,128)(2,1)S(1)} %copy-done, ...), kind=kOutput, calls=%fused_computation.15 | convolution fusion | flops 410910720 | bytes 3303936 | tf_op jit(solution)/shard_map/dot_general | solution.py:32
  44.0 1.1 copy.34
  45.1 1.1 copy.37
  46.2 1.1 copy.39
  47.4 1.1 copy.41
  48.5 1.1 copy.43
  49.7 1.1 copy.45
  50.8 1.1 copy.47
  51.9 1.4 exponential_reduce_fusion
  53.4 48.4 %all-reduce.5.cloned.1.call-done = f32[32,7,384]{0,1,2:T(8,128)} async-done(((f32[32,7,384]{0,1,2:T(8,128)}), f32[32,7,384]{0,1,2:T(8,128)}) %all-reduce.5.cloned.1.call-update) | async-done | bytes 344080 | tf_op jit(solution)/shard_map/psum | solution.py:12
  101.7 6.8 %fusion.32 = (f32[32,1,384]{0,1,2:T(1,128)S(1)}, f32[32,1,384]{0,1,2:T(1,128)S(1)}, f32[32,1,384]{0,1,2:T(1,128)S(1)}, f32[32,1,384]{0,1,2:T(1,128)S(1)}, f32[32...) fusion(f32[32,7,384]{0,1,2:T(8,128)} %all-reduce.5.cloned.1.call-done), kind=kLoop, calls=%fused_computation.44 | loop fusion | bytes 688128 | tf_op jit(solution)/shard_map/slice | solution.py:77
  108.5 0.1 copy.35
  108.6 0.1 copy.36
  108.7 0.1 copy.38
  108.8 0.1 copy.40
  108.9 0.1 copy.42
  109.1 0.1 copy.44
  109.2 0.1 copy.46
  109.3 0.0 copy-start.1
  109.3 98.8 %multiply_reduce_fusion = (f32[32,768]{1,0:T(8,128)}, f32[32,768]{1,0:T(8,128)}) fusion(s32[32,384,768]{2,1,0:T(8,128)} %param.12, f32[32,768]{1,0:T(8,128)S(1)} %copy.47, f32[32,384]{1,0:T(8,128)S(1)} %copy.46, f32[32,768]{1,0:T(8,128)S(1)} %copy.45, f32[32,384]{1,0:T(8,128)S(1)} %copy.44, f32[32,768]{1,0:T(8,128)S(1)} %copy.43, f32[32,384]{1,0:T(8,128)S(1)} %copy.42, ...), kind=kLoop, calls=%fused_computation.1 | loop fusion | flops 471810048 | bytes 38977536 | tf_op jit(solution)/shard_map/reduce_sum | solution.py:78
  208.1 0.0 all-reduce.7.cloned.1.call-update
  208.2 53.1 %all-reduce.7.cloned.1.call-done = (f32[32,768]{1,0:T(8,128)}, f32[32,768]{1,0:T(8,128)}) async-done(((f32[32,768]{1,0:T(8,128)}, f32[32,768]{1,0:T(8,128)}), (f32[32,768]{1,0:T(8,128)}, f32[32,768]{1,0:T(8,128)})) %all-reduce.7.cloned.1.call-update) | async-done | bytes 196624 | tf_op jit(solution)/shard_map/psum | solution.py:80
  261.3 0.9 maximum_divide_fusion
  262.1 0.0 copy-start.2
  262.1 0.4 fusion.33
  262.6 0.0 copy-done.1
  262.6 1.3 fusion.30
  263.9 39.6 %all-reduce = (f32[]{:T(128)}, f32[]{:T(128)}) all-reduce(f32[]{:T(128)} %get-tuple-element.12, f32[]{:T(128)} %get-tuple-element.28), channel_id=1, replica_groups=mesh['row'=4,'col'=8] {'row','col'}, use_global_device_ids=true, to_apply=%region_11.12 | all-reduce | flops 2 | bytes 16 | tf_op jit(solution)/shard_map/psum | solution.py:87
  304.7 0.0 copy-done.2
  (3 shorter events, 0.0 us)
Async XLA Ops:
  7.2 33.6 %copy-start = (bf16[384,128]{1,0:T(8,128)(2,1)S(1)}, bf16[384,128]{1,0:T(8,128)(2,1)}, u32[]{:S(2)}) copy-start(bf16[384,128]{1,0:T(8,128)(2,1)} %param.18) | copy-start | bytes 294916
  7.2 94.6 %all-reduce.5.cloned.1.call-start = ((), (), s32[]{:S(2)}) async-start(), calls=%async_computation | async-start | bytes 3145728 | tf_op jit(solution)/shard_map/psum | solution.py:12
  32.3 228.9 %all-reduce.7.cloned.1.call-start = ((), (), s32[]{:S(2)}) async-start(), calls=%async_computation.1 | async-start | bytes 393216 | tf_op jit(solution)/shard_map/psum | solution.py:80
  109.3 153.3 %copy-start.1 = (s32[32,96]{1,0:T(8,128)S(1)}, s32[32,96]{1,0:T(8,128)}, u32[]{:S(2)}) copy-start(s32[32,96]{1,0:T(8,128)} %param.15) | copy-start | bytes 36868
  262.1 42.6 %copy-start.2 = (f32[32,96]{1,0:T(8,128)}, f32[32,96]{1,0:T(8,128)S(1)}, u32[]{:S(2)}) copy-start(f32[32,96]{1,0:T(8,128)S(1)} %maximum_divide_fusion) | copy-start | bytes 36868
Sparse Core Ops, SparseCore 0:
  32.5 69.2 all-reduce.4
  208.3 52.9 all-reduce.6
where the time goes:
time: 314 us; the launch traced here: 313 us
  other arithmetic  109 us (35%)
  waiting for transfers between devices  102 us (32%)
  blocking collectives  60.8 us (19%)
  local copies, waits for them, and re-layouts  19.7 us (6%)
  between operations  16.6 us (5%)
  matrix products  4.59 us (1%)
    reduce_sum x1, other arithmetic, local(): preserved = jnp.sum(weights * scores, axis=1)  98.8 us
    psum x1, waiting for transfers between devices, local(): preserved_all, neighbors_all = lax.psum((preserved, neighbors), 'col')  53.1 us
    psum x1, waiting for transfers between devices, from_root(): return lax.psum(jnp.where(mine, shard, jnp.zeros_like(shard)), axis)  48.4 us
    psum x1, blocking collectives, local(): lax.psum((jnp.sum(residue_loss), jnp.sum(valid)), ('row', 'col'))  39.6 us
    all_gather x1, blocking collectives, local(): rows_part = lax.all_gather(stacked, 'col', axis=2, tiled=True)  21.3 us
    slice x1, local copies, waits for them, and re-layouts, local(): cols_part[:, 6, :, None]  6.78 us
  transfers between devices with their start and end apart: 2, of which 2 were waited for; matrix products, arithmetic and copies ran while one was open for 7% of the time, Pallas kernels for 0%

commit v1 on v0

--- a/solution.py
+++ b/solution.py
@@ -5,6 +5,13 @@
 
 L = 3072
 THRESHOLDS = (0.5, 1.0, 2.0, 4.0)
+
+
+def exchange_gather(shard, name, along):
+    count = lax.axis_size(name)
+    tiles = jnp.stack([shard for _ in range(count)])
+    tiles = lax.all_to_all(tiles, name, split_axis=0, concat_axis=0)
+    return jnp.concatenate(tiles, axis=along)
 
 
 def from_root(shard, axis, root):
@@ -62,7 +69,7 @@
     rows_len = L // row_count
     cols_len = L // col_count
     col_index = lax.axis_index("col")
-    rows_part = lax.all_gather(stacked, "col", axis=2, tiled=True)
+    rows_part = exchange_gather(stacked, "col", 2)
     offset = col_index * cols_len % rows_len
     column_piece = lax.dynamic_slice_in_dim(rows_part, offset, cols_len, 2)
     source_row = col_index * cols_len // rows_len

time: 314 us -> 273 us (0.87)
  blocking collectives: 60.8 us -> 39.6 us
  local copies, waits for them, and re-layouts: 19.7 us -> 2.91 us
  waiting for transfers between devices: 102 us -> 94 us
  starting transfers between devices: 0.08 us -> 5.28 us
    all_gather x1 -> x0, blocking collectives: 21.3 us -> none  [local(): rows_part = lax.all_gather(stacked, 'col', axis=2, tiled=True)]
    psum x1, waiting for transfers between devices: 48.4 us -> 34.5 us  [from_root(): return lax.psum(jnp.where(mine, shard, jnp.zeros_like(shard)), axis)]
    slice x2 -> x0, local copies, waits for them, and re-layouts: 10 us -> none  [the longest x1 6.78 us: local(): cols_part[:, 6, :, None]]
    sub x12 -> x0, local copies, waits for them, and re-layouts: 7.5 us -> none  [the longest x4 2.5 us: tile_dist(): total = total + (cols_block[:, 1, :, None] - rows_block[:, 1, None, :]) ** 2]
    all_to_all x0 -> x1, waiting for transfers between devices: none -> 5.61 us  [exchange_gather(): tiles = lax.all_to_all(tiles, name, split_axis=0, concat_axis=0)]
    all_to_all x0 -> x1, starting transfers between devices: none -> 5.2 us  [exchange_gather(): tiles = lax.all_to_all(tiles, name, split_axis=0, concat_axis=0)]
  transfers between devices with their start and end apart: 2 -> 3, of which waited for: 2 -> 3; matrix products, arithmetic and copies ran while one was open for 7% -> 4% of each run, Pallas kernels for 0% -> 0%
where the time goes in v1:
time: 273 us; the launch traced here: 272 us
  other arithmetic  109 us (40%)
  waiting for transfers between devices  94 us (34%)
  blocking collectives  39.6 us (15%)
  between operations  16.6 us (6%)
  starting transfers between devices  5.28 us (2%)
  matrix products  4.58 us (2%)
  local copies, waits for them, and re-layouts  2.91 us (1%)
    reduce_sum x1, other arithmetic, local(): preserved = jnp.sum(weights * scores, axis=1)  98.8 us
    psum x1, waiting for transfers between devices, local(): preserved_all, neighbors_all = lax.psum((preserved, neighbors), 'col')  53.8 us
    psum x1, blocking collectives, local(): lax.psum((jnp.sum(residue_loss), jnp.sum(valid)), ('row', 'col'))  39.6 us
    psum x1, waiting for transfers between devices, from_root(): return lax.psum(jnp.where(mine, shard, jnp.zeros_like(shard)), axis)  34.5 us
    all_to_all x1, waiting for transfers between devices, exchange_gather(): tiles = lax.all_to_all(tiles, name, split_axis=0, concat_axis=0)  5.61 us
  transfers between devices with their start and end apart: 3, of which 3 were waited for; matrix products, arithmetic and copies ran while one was open for 4% of the time, Pallas kernels for 0%

profile of v1, /device:TPU:0, one launch (start us, length us, event | category | flops | bytes accessed | tf_op | source)
XLA Modules:
  0.0 271.9 jit_solution(17500677256714118818)
XLA Ops:
  7.2 0.0 copy-start
  7.2 0.8 convert_bitcast_fusion
  7.9 0.8 pad_maximum_fusion
  8.8 1.0 stack.2
  9.8 5.2 %all-to-all-start = ((f32[8,32,7,96]{3,1,2,0:T(8,128)}), f32[8,32,7,96]{3,1,2,0:T(8,128)S(1)}, u32[]{:S(2)}, u32[]{:S(2)}) async-start(f32[8,32,7,96]{3,1,2,0:T(8,128)} %stack.2), calls=%async_computation | async-start | bytes 1835008 | tf_op jit(solution)/shard_map/all_to_all | solution.py:13
  15.0 0.0 all-reduce.5.cloned.1.call-start
  15.1 2.3 convert_reduce_fusion
  17.4 2.8 %fusion.4 = f32[32,96]{1,0:T(8,128)S(1)} fusion(bf16[32,96,384]{2,1,0:T(8,128)(2,1)} %param.16, f32[32,96]{1,0:T(8,128)S(1)} %broadcast_multiply_fusion), kind=kLoop, calls=%fused_computation.8 | loop fusion | flops 4715520 | bytes 2383872 | tf_op jit(solution)/shard_map/reduce_sum | solution.py:33
  20.2 0.0 copy-done
  20.2 3.2 %maximum_convert_fusion = bf16[32,96,128]{2,1,0:T(8,128)(2,1)S(1)} fusion(bf16[32,96,384]{2,1,0:T(8,128)(2,1)} %param.16, f32[384]{0:T(512)} %param.17, f32[32,96]{1,0:T(8,128)S(1)} %add_rsqrt_fusion, f32[32,96]{1,0:T(8,128)S(1)} %broadcast_multiply_fusion, f32[128]{0:T(128)} %param.21, f32[128]{0:T(128)} %param.19, bf16[384,128]{1,0:T(8,128)(2,1)S(1)} %copy-done, ...), kind=kOutput, calls=%fused_computation.15 | convolution fusion | flops 410910720 | bytes 3303936 | tf_op jit(solution)/shard_map/dot_general | solution.py:39
  23.4 5.6 %all-to-all-done = f32[8,32,7,96]{3,1,2,0:T(8,128)S(1)} async-done(((f32[8,32,7,96]{3,1,2,0:T(8,128)}), f32[8,32,7,96]{3,1,2,0:T(8,128)S(1)}, u32[]{:S(2)}, u32[]{:S(2)}) %all-to-all-start) | async-done | bytes 688160 | tf_op jit(solution)/shard_map/all_to_all | solution.py:13
  29.0 0.5 copy.15
  29.5 0.3 reshape.46
  29.8 0.9 dynamic-slice_select_fusion
  30.7 0.0 all-reduce.5.cloned.1.call-update
  30.8 0.0 all-reduce.7.cloned.1.call-start
  30.8 1.4 exponential_reduce_fusion
  32.3 34.5 %all-reduce.5.cloned.1.call-done = f32[32,7,384]{2,0,1:T(8,128)} async-done(((f32[32,7,384]{2,0,1:T(8,128)}), f32[32,7,384]{2,0,1:T(8,128)}) %all-reduce.5.cloned.1.call-update) | async-done | bytes 344080 | tf_op jit(solution)/shard_map/psum | solution.py:19
  66.8 1.0 slice_bitcast_fusion.13
  67.8 0.0 copy-start.1
  67.8 98.8 %multiply_reduce_fusion = (f32[32,768]{1,0:T(8,128)}, f32[32,768]{1,0:T(8,128)}) fusion(s32[32,384,768]{2,1,0:T(8,128)} %param.12, f32[32,768]{1,0:T(8,128)S(1)} %get-tuple-element.12, f32[32,384]{1,0:T(8,128)S(1)} %get-tuple-element.19, f32[32,768]{1,0:T(8,128)S(1)} %get-tuple-element.13, f32[32,384]{1,0:T(8,128)S(1)} %get-tuple-element.20, ...), kind=kLoop, calls=%fused_computation.1 | loop fusion | flops 471810048 | bytes 38977536 | tf_op jit(solution)/shard_map/reduce_sum | solution.py:85
  166.7 0.0 all-reduce.7.cloned.1.call-update
  166.7 53.8 %all-reduce.7.cloned.1.call-done = (f32[32,768]{1,0:T(8,128)}, f32[32,768]{1,0:T(8,128)}) async-done(((f32[32,768]{1,0:T(8,128)}, f32[32,768]{1,0:T(8,128)}), (f32[32,768]{1,0:T(8,128)}, f32[32,768]{1,0:T(8,128)})) %all-reduce.7.cloned.1.call-update) | async-done | bytes 196624 | tf_op jit(solution)/shard_map/psum | solution.py:87
  220.5 0.9 maximum_divide_fusion
  221.3 0.0 copy-start.2
  221.4 0.4 fusion.31
  221.8 0.0 copy-done.1
  221.8 1.3 fusion.30
  223.1 39.6 %all-reduce = (f32[]{:T(128)}, f32[]{:T(128)}) all-reduce(f32[]{:T(128)} %get-tuple-element.9, f32[]{:T(128)} %get-tuple-element.25), channel_id=1, replica_groups=mesh['row'=4,'col'=8] {'row','col'}, use_global_device_ids=true, to_apply=%region_11.12 | all-reduce | flops 2 | bytes 16 | tf_op jit(solution)/shard_map/psum | solution.py:94
  263.9 0.0 copy-done.2
  (4 shorter events, 0.1 us)
Async XLA Ops:
  7.2 13.0 %copy-start = (bf16[384,128]{1,0:T(8,128)(2,1)S(1)}, bf16[384,128]{1,0:T(8,128)(2,1)}, u32[]{:S(2)}) copy-start(bf16[384,128]{1,0:T(8,128)(2,1)} %param.18) | copy-start | bytes 294916
  9.8 19.2 %all-to-all-start = ((f32[8,32,7,96]{3,1,2,0:T(8,128)}), f32[8,32,7,96]{3,1,2,0:T(8,128)S(1)}, u32[]{:S(2)}, u32[]{:S(2)}) async-start(f32[8,32,7,96]{3,1,2,0:T(8,128)} %stack.2), calls=%async_computation | async-start | bytes 1835008 | tf_op jit(solution)/shard_map/all_to_all | solution.py:13
  15.0 51.8 %all-reduce.5.cloned.1.call-start = ((), (), s32[]{:S(2)}) async-start(), calls=%async_computation.1 | async-start | bytes 688128 | tf_op jit(solution)/shard_map/psum | solution.py:19
  30.8 189.7 %all-reduce.7.cloned.1.call-start = ((), (), s32[]{:S(2)}) async-start(), calls=%async_computation.2 | async-start | bytes 393216 | tf_op jit(solution)/shard_map/psum | solution.py:87
  67.8 154.0 %copy-start.1 = (s32[32,96]{1,0:T(8,128)S(1)}, s32[32,96]{1,0:T(8,128)}, u32[]{:S(2)}) copy-start(s32[32,96]{1,0:T(8,128)} %param.15) | copy-start | bytes 36868
  221.3 42.6 %copy-start.2 = (f32[32,96]{1,0:T(8,128)}, f32[32,96]{1,0:T(8,128)S(1)}, u32[]{:S(2)}) copy-start(f32[32,96]{1,0:T(8,128)S(1)} %maximum_divide_fusion) | copy-start | bytes 36868
Sparse Core Ops, SparseCore 0:
  30.9 35.9 all-reduce.4
  166.8 53.6 all-reduce.6
